TPU v7x, 32 devices: a 4x4x1 block of a 4x4x8 slice. The times are simulated.
32 devices in a mesh: dp: 1 (over z), tp: 32 (over y, x, core).
Axes of the slice: x: 4, y: 4, z: 1, core: 2. Of those that a mesh axis runs over, the one named last changes fastest.
The devices are a block of a 4x4x8 slice.
Arguments:
- x: bfloat16 [192, 2048], P('dp')
- lengths: int32 [65], P('dp')
- attn_gain: bfloat16 [2, 2048], replicated
- w_q: bfloat16 [2, 2048, 2048], P(None, None, 'tp')
- w_k: bfloat16 [2, 2048, 2048], P(None, None, 'tp')
- w_v: bfloat16 [2, 2048, 2048], P(None, None, 'tp')
- w_o: bfloat16 [2, 2048, 2048], P(None, 'tp')
- mlp_gain: bfloat16 [2, 2048], replicated
- w_gate: bfloat16 [2, 2048, 8192], P(None, None, 'tp')
- w_up: bfloat16 [2, 2048, 8192], P(None, None, 'tp')
- w_down: bfloat16 [2, 8192, 2048], P(None, 'tp')
- k_cache: bfloat16 [2, 65, 32, 1024, 64], P(None, 'dp', 'tp')
- v_cache: bfloat16 [2, 65, 32, 1024, 64], P(None, 'dp', 'tp')
Outputs:
- output: bfloat16 [192, 2048], P('dp')
All inputs are finite; a program needn't handle non-finite values.
Results may differ from a plain program's by a relative error of at most 0.02.
Values are sent between devices in bfloat16 or wider.
A program may use at most 768 MiB of HBM per device.

v0:
```python
import jax
import jax.numpy as jnp
from jax import lax
from jax.sharding import PartitionSpec as P

ROPE_BASE = 500000.0
EPSILON = 1e-5


def rms_norm(x, norm_gain):
    x_f32 = x.astype(jnp.float32)
    inv_rms = lax.rsqrt(jnp.mean(x_f32 * x_f32, axis=-1, keepdims=True) + EPSILON)
    return (x_f32 * inv_rms * norm_gain.astype(jnp.float32)).astype(jnp.bfloat16)


def rope_tables(positions, head_dim):
    freq_exps = jnp.arange(0, head_dim, 2, dtype=jnp.float32) / head_dim
    angles = positions.astype(jnp.float32)[:, None] * jnp.power(ROPE_BASE, -freq_exps)[None, :]
    return jnp.cos(angles)[:, None, :], jnp.sin(angles)[:, None, :]


def apply_rope(vectors, cos_tab, sin_tab):
    half_dim = vectors.shape[-1] // 2
    vec_f32 = vectors.astype(jnp.float32)
    first = vec_f32[..., :half_dim]
    second = vec_f32[..., half_dim:]
    return jnp.concatenate([first * cos_tab - second * sin_tab, second * cos_tab + first * sin_tab], axis=-1).astype(jnp.bfloat16)


def project(normed, weight, head_dim):
    return jnp.dot(normed, weight, preferred_element_type=jnp.float32).astype(jnp.bfloat16).reshape(normed.shape[0], -1, head_dim)


def attention(q_rot, k_rot, v_new, k_cache, v_cache, lengths):
    dec_rows = lengths.shape[0] - 1
    kv_local = k_cache.shape[1]
    seq_len = k_cache.shape[2]
    head_dim = k_cache.shape[3]
    tok_count = q_rot.shape[0]
    chunk_len = tok_count - dec_rows
    attn_scale = head_dim ** -0.5
    q_grouped = q_rot.reshape(tok_count, kv_local, -1, head_dim)
    q_dec = q_grouped[:dec_rows]
    q_chk = q_grouped[dec_rows:]
    seq_ids = jnp.arange(seq_len)
    dec_cache = jnp.einsum('bgrd,bgsd->bgrs', q_dec, k_cache[:dec_rows], preferred_element_type=jnp.float32) * attn_scale
    dec_cache = jnp.where(seq_ids[None, None, None, :] < lengths[:dec_rows, None, None, None], dec_cache, -jnp.inf)
    dec_self = jnp.einsum('bgrd,bgd->bgr', q_dec, k_rot[:dec_rows], preferred_element_type=jnp.float32)[..., None] * attn_scale
    dec_prob = jax.nn.softmax(jnp.concatenate([dec_cache, dec_self], axis=-1), axis=-1).astype(jnp.bfloat16)
    dec_out = jnp.einsum('bgrs,bgsd->bgrd', dec_prob[..., :seq_len], v_cache[:dec_rows], preferred_element_type=jnp.float32) + dec_prob[..., seq_len:].astype(jnp.float32) * v_new[:dec_rows, :, None, :].astype(jnp.float32)
    chk_cache = jnp.einsum('cgrd,gsd->cgrs', q_chk, k_cache[dec_rows], preferred_element_type=jnp.float32) * attn_scale
    chk_cache = jnp.where(seq_ids[None, None, None, :] < lengths[dec_rows], chk_cache, -jnp.inf)
    chk_self = jnp.einsum('cgrd,jgd->cgrj', q_chk, k_rot[dec_rows:], preferred_element_type=jnp.float32) * attn_scale
    tok_ids = jnp.arange(chunk_len)
    causal_mask = tok_ids[None, :] <= tok_ids[:, None]
    chk_self = jnp.where(causal_mask[:, None, None, :], chk_self, -jnp.inf)
    chk_prob = jax.nn.softmax(jnp.concatenate([chk_cache, chk_self], axis=-1), axis=-1).astype(jnp.bfloat16)
    chk_out = jnp.einsum('cgrs,gsd->cgrd', chk_prob[..., :seq_len], v_cache[dec_rows], preferred_element_type=jnp.float32) + jnp.einsum('cgrj,jgd->cgrd', chk_prob[..., seq_len:], v_new[dec_rows:], preferred_element_type=jnp.float32)
    return jnp.concatenate([dec_out.reshape(dec_rows, -1), chk_out.reshape(chunk_len, -1)], axis=0).astype(jnp.bfloat16)


def decoder_layer(x, cos_tab, sin_tab, lengths, attn_gain, w_q, w_k, w_v, w_o, mlp_gain, w_gate, w_up, w_down, k_cache, v_cache):
    head_dim = k_cache.shape[-1]
    normed = rms_norm(x, attn_gain)
    q_rot = apply_rope(project(normed, w_q, head_dim), cos_tab, sin_tab)
    k_rot = apply_rope(project(normed, w_k, head_dim), cos_tab, sin_tab)
    v_new = project(normed, w_v, head_dim)
    attended = attention(q_rot, k_rot, v_new, k_cache, v_cache, lengths)
    attn_part = jnp.dot(attended, w_o, preferred_element_type=jnp.float32).astype(jnp.bfloat16)
    attn_sum = lax.psum(attn_part, 'tp')
    hidden = (x.astype(jnp.float32) + attn_sum.astype(jnp.float32)).astype(jnp.bfloat16)
    mlp_in = rms_norm(hidden, mlp_gain)
    gate_proj = jnp.dot(mlp_in, w_gate, preferred_element_type=jnp.float32)
    up_proj = jnp.dot(mlp_in, w_up, preferred_element_type=jnp.float32)
    activated = (jax.nn.silu(gate_proj) * up_proj).astype(jnp.bfloat16)
    mlp_part = jnp.dot(activated, w_down, preferred_element_type=jnp.float32).astype(jnp.bfloat16)
    mlp_sum = lax.psum(mlp_part, 'tp')
    return (hidden.astype(jnp.float32) + mlp_sum.astype(jnp.float32)).astype(jnp.bfloat16)


def solution(mesh):
    col_spec = P(None, None, 'tp')
    row_spec = P(None, 'tp', None)
    cache_spec = P(None, 'dp', 'tp', None, None)
    in_specs = (P('dp', None), P('dp'), P(), col_spec, col_spec, col_spec, row_spec, P(), col_spec, col_spec, row_spec, cache_spec, cache_spec)

    def body(x, lengths, attn_gain, w_q, w_k, w_v, w_o, mlp_gain, w_gate, w_up, w_down, k_cache, v_cache):
        dec_rows = lengths.shape[0] - 1
        chunk_len = x.shape[0] - dec_rows
        positions = jnp.concatenate([lengths[:dec_rows], lengths[dec_rows] + jnp.arange(chunk_len, dtype=jnp.int32)])
        cos_tab, sin_tab = rope_tables(positions, k_cache.shape[-1])
        hidden = x
        for layer_idx in range(w_q.shape[0]):
            hidden = decoder_layer(hidden, cos_tab, sin_tab, lengths, attn_gain[layer_idx], w_q[layer_idx], w_k[layer_idx], w_v[layer_idx], w_o[layer_idx], mlp_gain[layer_idx], w_gate[layer_idx], w_up[layer_idx], w_down[layer_idx], k_cache[layer_idx], v_cache[layer_idx])
        return hidden

    return jax.shard_map(body, mesh=mesh, in_specs=in_specs, out_specs=P('dp', None), check_vma=False)
```

profile of v0, /device:TPU:97, one launch (start us, length us, event | category | flops | bytes accessed | tf_op | source)
XLA Modules:
  0.0 453.0 jit_solution(17256701035630726383)
XLA Ops:
  6.6 1.3 slice.204
  7.9 0.6 iota_add_fusion
  8.6 0.7 iota_compare_fusion.2
  9.2 1.4 fusion
  10.6 0.8 slice_convert_fusion.3
  11.4 1.6 fusion.29
  13.1 0.4 fusion.27
  13.5 0.1 add_convert_fusion.2
  13.6 0.2 fusion.129
  13.9 0.4 fusion.190
  14.2 0.1 copy.47
  14.3 5.2 %multiply_reduce_fusion.3 = f32[64,1024]{1,0:T(8,128)S(1)} fusion(f32[64,64]{1,0:T(8,128)S(1)} %copy.47, bf16[2,65,1,1024,64]{3,4,2,1,0:T(8,128)(2,1)} %param.24), kind=kLoop, calls=%fused_computation.3 | loop fusion | flops 12517376 | bytes 8667136
  19.5 0.2 copy.20
  19.7 0.2 fusion.60
  19.9 0.2 fusion.67
  20.0 0.1 divide_convert_fusion.3
  20.2 0.5 copy-done.5
  20.7 0.4 convolution_convert_fusion.7
  21.2 0.2 copy.48
  21.4 5.1 %multiply_reduce_fusion.2 = f32[64,64]{1,0:T(8,128)S(1)} fusion(f32[64,1024]{1,0:T(8,128)S(1)} %copy.48, bf16[2,65,1,1024,64]{3,4,2,1,0:T(8,128)(2,1)} %param.25), kind=kLoop, calls=%fused_computation.2 | loop fusion | flops 12578816 | bytes 8667136
  26.4 0.1 copy.28
  26.5 1.4 fusion.189
  27.9 0.2 fusion.65
  28.1 0.2 divide_convert_fusion.1
  28.4 1.1 convolution_bitcast_fusion.1
  29.5 0.2 fusion.37
  29.7 1.3 convolution_convert_fusion.3
  31.1 0.1 all-reduce.7.cloned.1.call-start
  31.2 98.6 %all-reduce.5.cloned.1.call-done = bf16[192,2048]{1,0:T(8,128)(2,1)} async-done(((bf16[192,2048]{1,0:T(8,128)(2,1)}), bf16[192,2048]{1,0:T(8,128)(2,1)}) %all-reduce.5.cloned.1.call-update) | async-done | bytes 786448 | tf_op jit(solution)/shard_map/psum | solution.py:70
  129.8 1.6 fusion.4
  131.4 0.2 copy-done.9
  131.6 0.4 fusion.46
  132.0 3.5 convolution_convert_fusion.2
  135.6 0.2 all-reduce.9.cloned.1.call-start
  135.9 94.0 %all-reduce.7.cloned.1.call-done = bf16[192,2048]{1,0:T(8,128)(2,1)} async-done(((bf16[192,2048]{1,0:T(8,128)(2,1)}), bf16[192,2048]{1,0:T(8,128)(2,1)}) %all-reduce.7.cloned.1.call-update) | async-done | bytes 786448 | tf_op jit(solution)/shard_map/psum | solution.py:77
  229.8 1.5 fusion.8
  231.4 0.3 fusion.10
  231.7 0.7 copy-done.6
  232.4 0.4 convolution_convert_fusion.4
  232.8 0.4 fusion.33
  233.2 0.4 fusion.31
  233.6 0.2 fusion.137
  233.8 0.4 fusion.192
  234.2 0.1 copy.50
  234.3 5.2 %multiply_reduce_fusion.1 = f32[64,1024]{1,0:T(8,128)S(1)} fusion(f32[64,64]{1,0:T(8,128)S(1)} %copy.50, bf16[2,65,1,1024,64]{3,4,2,1,0:T(8,128)(2,1)} %param.24), kind=kLoop, calls=%fused_computation.1 | loop fusion | flops 12517376 | bytes 8667136
  239.5 0.2 copy.34
  239.7 0.2 fusion.62
  239.8 0.2 fusion.66
  240.0 0.1 divide_convert_fusion.2
  240.2 1.3 fusion.191
  241.5 0.2 copy.51
  241.7 5.1 %multiply_reduce_fusion = f32[64,64]{1,0:T(8,128)S(1)} fusion(f32[64,1024]{1,0:T(8,128)S(1)} %copy.51, bf16[2,65,1,1024,64]{3,4,2,1,0:T(8,128)(2,1)} %param.25), kind=kLoop, calls=%fused_computation | loop fusion | flops 12578816 | bytes 8667136
  246.7 0.1 copy.42
  246.8 0.2 fusion.64
  247.1 0.2 divide_convert_fusion
  247.3 1.1 convolution_bitcast_fusion
  248.4 0.2 fusion.36
  248.6 1.3 convolution_convert_fusion.1
  250.1 94.1 %all-reduce.9.cloned.1.call-done = bf16[192,2048]{1,0:T(8,128)(2,1)} async-done(((bf16[192,2048]{1,0:T(8,128)(2,1)}), bf16[192,2048]{1,0:T(8,128)(2,1)}) %all-reduce.9.cloned.1.call-update) | async-done | bytes 786448 | tf_op jit(solution)/shard_map/psum | solution.py:70
  344.2 1.8 fusion.12
  346.0 0.4 fusion.41
  346.4 3.5 convolution_convert_fusion
  350.0 94.2 %all-reduce.11.cloned.1.call-done = bf16[192,2048]{1,0:T(8,128)(2,1)} async-done(((bf16[192,2048]{1,0:T(8,128)(2,1)}), bf16[192,2048]{1,0:T(8,128)(2,1)}) %all-reduce.11.cloned.1.call-update) | async-done | bytes 786448 | tf_op jit(solution)/shard_map/psum | solution.py:77
  444.2 2.3 fusion.15
  (45 shorter events, 0.6 us)
Async XLA Ops:
  6.5 6.5 %copy-start.1 = (bf16[192,2048]{1,0:T(8,128)(2,1)S(1)}, bf16[192,2048]{1,0:T(8,128)(2,1)}, u32[]{:S(2)}) copy-start(bf16[192,2048]{1,0:T(8,128)(2,1)} %param.13) | copy-start | bytes 2359300
  6.5 6.5 %copy-start.4 = (bf16[2,2048,64]{1,2,0:T(8,128)(2,1)S(1)}, bf16[2,2048,64]{1,2,0:T(8,128)(2,1)}, u32[]{:S(2)}) copy-start(bf16[2,2048,64]{1,2,0:T(8,128)(2,1)} %param.16) | copy-start | bytes 1572868
  6.6 123.2 %all-reduce.5.cloned.1.call-start = ((), (), s32[]{:S(2)}) async-start(), calls=%async_computation | async-start | bytes 1572864 | tf_op jit(solution)/shard_map/psum | solution.py:70
  11.4 2.1 copy-start.8
  19.7 1.0 copy-start.5
  26.4 3.3 copy-start.2
  28.1 3.0 copy-start.7
  31.1 198.7 %all-reduce.7.cloned.1.call-start = ((), (), s32[]{:S(2)}) async-start(), calls=%async_computation.1 | async-start | bytes 1572864 | tf_op jit(solution)/shard_map/psum | solution.py:77
  129.8 1.8 copy-start.9
  135.6 208.6 %all-reduce.9.cloned.1.call-start = ((), (), s32[]{:S(2)}) async-start(), calls=%async_computation.2 | async-start | bytes 1572864 | tf_op jit(solution)/shard_map/psum | solution.py:70
  229.8 1.6 copy-start
  231.4 1.0 copy-start.6
  231.4 1.4 copy-start.3
  250.0 194.2 %all-reduce.11.cloned.1.call-start = ((), (), s32[]{:S(2)}) async-start(), calls=%async_computation.3 | async-start | bytes 1572864 | tf_op jit(solution)/shard_map/psum | solution.py:77
  344.2 1.8 copy-start.10
Sparse Core Ops, SparseCore 0:
  31.2 98.5 all-reduce.4
  135.7 94.0 all-reduce.6
  250.1 94.0 all-reduce.8
  350.1 94.0 all-reduce.10
where the time goes:
time: 454 us; the launch traced here: 453 us
  waiting for transfers between devices  381 us (84%)
  other arithmetic  34.1 us (8%)
  matrix products  20.2 us (4%)
  between operations  13.5 us (3%)
    psum x2, waiting for transfers between devices, decoder_layer(): attn_sum = lax.psum(attn_part, 'tp')  193 us
    psum x2, waiting for transfers between devices, decoder_layer(): mlp_sum = lax.psum(mlp_part, 'tp')  188 us
    unnamed x8, other arithmetic  20.6 us
  transfers between devices with their start and end apart: 4, of which 4 were waited for; matrix products, arithmetic and copies ran while one was open for 0% of the time, Pallas kernels for 0%

commit v1 on v0

v1 whole, which is shorter than its diff:
```python
import functools

import jax
import jax.numpy as jnp
from jax import lax
from jax.experimental import pallas as pl
from jax.experimental.pallas import tpu as pltpu
from jax.sharding import PartitionSpec as P

ROPE_BASE = 500000.0
EPSILON = 1e-5
MESH = pl.DeviceIdType.MESH
LANES = 128
BLOCK = 16
F32 = jnp.float32
BF16 = jnp.bfloat16


def rope_tables(positions, head_dim):
    freq_exps = jnp.arange(0, head_dim, 2, dtype=F32) / head_dim
    angles = positions.astype(F32)[:, None] * jnp.power(ROPE_BASE, -freq_exps)[None, :]
    cos, sin = jnp.cos(angles), jnp.sin(angles)
    return jnp.concatenate([cos, cos, cos, cos], axis=1), jnp.concatenate([-sin, sin, -sin, sin], axis=1)


def tables(lengths, tok, head_dim, gains):
    dec = lengths.shape[0] - 1
    positions = jnp.concatenate([lengths[:dec], lengths[dec] + jnp.arange(tok - dec, dtype=jnp.int32)])
    cos_tab, sin_tab = rope_tables(positions, head_dim)
    len_tab = jnp.broadcast_to(jnp.concatenate([lengths[:dec], jnp.broadcast_to(lengths[dec:], (8,))])[:, None], (dec + 8, LANES))
    return len_tab, cos_tab, sin_tab, gains.astype(F32).reshape(-1, LANES)


def nt_dot(a, b):
    return lax.dot_general(a, b, (((1,), (1,)), ((), ())), preferred_element_type=F32)


def layers_kernel(dims, x_hbm, len_ref, cos_ref, sin_ref, gain_ref, wq_hbm, wk_hbm, wv_hbm, wo_hbm, wg_hbm, wu_hbm, wd_hbm, kc_hbm, vc_hbm, out_hbm,
                  hbuf, part, pair_in, mine, rs_in, normed, qkv, qbd, logits, probs, attended, act,
                  wqkv, wo, wg, wu, wd, kc, vc,
                  x_sem, w_sem, out_sem, pair_send, pair_recv, rs_send, rs_recv, ag_send, ag_recv, fwd_send, fwd_recv):
    n, layers, tok, width, dec, seq, hd, ff = dims
    chips = n // 2
    side = int(round(chips ** 0.5))
    half = tok // 2
    chunk = tok - dec
    ncol = width // LANES
    me = lax.axis_index("tp")
    core = lax.rem(me, 2)
    chip = me // 2
    my_y, my_x = chip // side, lax.rem(chip, side)
    partner = chip * 2 + (1 - core)
    my_rows = pl.ds(pl.multiple_of(core * half, half), half)
    other_rows = pl.ds(pl.multiple_of((1 - core) * half, half), half)

    def peer_chip(step):
        return lax.rem(my_y + step // side, side) * side + lax.rem(my_x + lax.rem(step, side), side)

    barrier = pltpu.get_barrier_semaphore()
    pl.semaphore_signal(barrier, inc=1, device_id={"tp": partner}, device_id_type=MESH)

    def greet(step, carry):
        pl.semaphore_signal(barrier, inc=1, device_id={"tp": peer_chip(step) * 2 + core}, device_id_type=MESH)
        return carry

    lax.fori_loop(1, chips, greet, 0)

    def x_copy(c):
        return pltpu.make_async_copy(x_hbm.at[:, pl.ds(c * LANES, LANES)], hbuf.at[c], x_sem.at[c])

    def load(l, name):
        i, src, dst = {
            "q": (0, wq_hbm, wqkv.at[l, pl.ds(0, hd)]),
            "k": (1, wk_hbm, wqkv.at[l, pl.ds(hd, hd)]),
            "v": (2, wv_hbm, wqkv.at[l, pl.ds(2 * hd, hd)]),
            "o": (3, wo_hbm, wo.at[l]),
            "gate": (4, wg_hbm, wg.at[l]),
            "up": (5, wu_hbm, wu.at[l]),
            "down": (6, wd_hbm, wd.at[l]),
            "keys": (7, kc_hbm, kc.at[l]),
            "values": (8, vc_hbm, vc.at[l]),
        }[name]
        return pltpu.make_async_copy(src.at[l], dst, w_sem.at[l, i])

    def load_all(l):
        for name in ("q", "k", "v", "keys", "values", "o", "gate", "up", "down"):
            load(l, name).start()

    for c in range(ncol):
        x_copy(c).start()
    load_all(0)
    for c in range(ncol):
        x_copy(c).wait()

    def norm(gain_row):
        def square(c, acc):
            h = hbuf[c].astype(F32)
            return acc + h * h

        total = lax.fori_loop(0, ncol, square, jnp.zeros((tok, LANES), F32))
        inv = lax.rsqrt(jnp.sum(total, axis=1, keepdims=True) / width + EPSILON)

        def scale(c, carry):
            gain = gain_ref[pl.ds(gain_row * ncol + c, 1), :]
            normed[:, pl.ds(pl.multiple_of(c * LANES, LANES), LANES)] = (hbuf[c].astype(F32) * inv * gain).astype(BF16)
            return carry

        lax.fori_loop(0, ncol, scale, 0)

    def attention(l):
        for name in ("q", "k", "v"):
            load(l, name).wait()
        proj = nt_dot(normed[...], wqkv[l]).astype(BF16)
        lane = lax.broadcasted_iota(jnp.int32, (tok, LANES), 1)
        qk = proj[:, :2 * hd].astype(F32)
        turned = jnp.where(lax.rem(lane, hd) < hd // 2, pltpu.roll(qk, LANES - hd // 2, 1), pltpu.roll(qk, hd // 2, 1))
        qk = (qk * cos_ref[...] + turned * sin_ref[...]).astype(BF16).astype(F32)
        qkv[:, :2 * hd] = qk.astype(BF16)
        qkv[:, 2 * hd:3 * hd] = proj[:, 2 * hd:]
        qk_dec = qk[:dec]
        q_twice = jnp.where(lane[:dec] < hd, qk_dec, pltpu.roll(qk_dec, hd, 1))
        row = lax.rem(lax.broadcasted_iota(jnp.int32, (dec, LANES), 0), BLOCK)
        for j in range(BLOCK * hd // LANES):
            keep = row == 2 * j + lane[:dec] // hd
            qbd[:, j * LANES:(j + 1) * LANES] = jnp.where(keep, q_twice, 0.0).astype(BF16)
        k_twice = jnp.where(lane[:dec] < hd, pltpu.roll(qk_dec, hd, 1), qk_dec)
        scale = hd ** -0.5
        self_logit = jnp.sum(jnp.where(lane[:dec] < hd, q_twice * k_twice, 0.0), axis=1, keepdims=True) * scale
        load(l, "keys").wait()
        span = BLOCK * hd

        def dec_logits(g, carry):
            rows = pl.ds(pl.multiple_of(g * BLOCK, BLOCK), BLOCK)
            keys = kc[l, pl.ds(pl.multiple_of(g * span, span), span), :]
            logits[rows, :] = jnp.dot(qbd[rows, :], keys, preferred_element_type=F32)
            return carry

        lax.fori_loop(0, dec // BLOCK, dec_logits, 0)
        lens = len_ref[0:dec, 0:1]
        pos = lax.broadcasted_iota(jnp.int32, (dec, seq), 1)
        lg = jnp.where(pos < lens, logits[0:dec, :] * scale, -jnp.inf)
        top = jnp.maximum(jnp.max(lg, axis=1, keepdims=True), self_logit)
        ex = jnp.exp(lg - top)
        ex_self = jnp.exp(self_logit - top)
        inv = 1.0 / (jnp.sum(ex, axis=1, keepdims=True) + ex_self)
        probs[0:dec, :] = (ex * inv).astype(BF16)
        p_self = (ex_self * inv).astype(BF16).astype(F32)
        q_chk = qkv[dec:, 0:hd]
        lg = jnp.dot(q_chk, kc[l, dec * hd:(dec + 1) * hd, :], preferred_element_type=F32) * scale
        lg_new = nt_dot(q_chk, qkv[dec:, hd:2 * hd]) * scale
        pos = lax.broadcasted_iota(jnp.int32, (chunk, seq), 1)
        lg = jnp.where(pos < len_ref[dec:dec + 1, 0:1], lg, -jnp.inf)
        tok_r = lax.broadcasted_iota(jnp.int32, (chunk, chunk), 0)
        tok_c = lax.broadcasted_iota(jnp.int32, (chunk, chunk), 1)
        lg_new = jnp.where(tok_c <= tok_r, lg_new, -jnp.inf)
        top = jnp.maximum(jnp.max(lg, axis=1, keepdims=True), jnp.max(lg_new, axis=1, keepdims=True))
        ex, ex_new = jnp.exp(lg - top), jnp.exp(lg_new - top)
        inv = 1.0 / (jnp.sum(ex, axis=1, keepdims=True) + jnp.sum(ex_new, axis=1, keepdims=True))
        probs[dec:, :] = (ex * inv).astype(BF16)
        p_new = (ex_new * inv).astype(BF16)
        load(l, "values").wait()
        lane_b = lax.broadcasted_iota(jnp.int32, (BLOCK, LANES), 1)
        row_b = lax.broadcasted_iota(jnp.int32, (BLOCK, LANES), 0)

        def dec_values(g, carry):
            rows = pl.ds(pl.multiple_of(g * BLOCK, BLOCK), BLOCK)
            full = nt_dot(probs[rows, :], vc[l, pl.ds(pl.multiple_of(g * span, span), span), :])
            acc = jnp.zeros((BLOCK, LANES), F32)
            for j in range(BLOCK * hd // LANES):
                acc += jnp.where(row_b == 2 * j + lane_b // hd, full[:, j * LANES:(j + 1) * LANES], 0.0)
            logits[rows, 0:LANES] = acc + pltpu.roll(acc, hd, 1)
            return carry

        lax.fori_loop(0, dec // BLOCK, dec_values, 0)
        attended[0:dec, :] = (logits[0:dec, 0:hd] + p_self * qkv[0:dec, 2 * hd:3 * hd].astype(F32)).astype(BF16)
        out = nt_dot(probs[dec:, :], vc[l, dec * hd:(dec + 1) * hd, :])
        out += jnp.dot(p_new, qkv[dec:, 2 * hd:3 * hd], preferred_element_type=F32)
        attended[dec:, :] = out.astype(BF16)
        load(l, "o").wait()
        project_out(attended, wo.at[l])

    def project_out(lhs_ref, w_ref):
        lhs = lhs_ref[...]
        for c in range(0, ncol, 4):
            out = jnp.dot(lhs, w_ref[:, c * LANES:(c + 4) * LANES], preferred_element_type=F32).astype(BF16)
            for j in range(4):
                part[c + j] = out[:, j * LANES:(j + 1) * LANES]

    def mlp(l):
        for name in ("gate", "up", "down"):
            load(l, name).wait()
        a = normed[...]
        gate = jnp.dot(a, wg[l], preferred_element_type=F32)
        up = jnp.dot(a, wu[l], preferred_element_type=F32)
        act[...] = (gate * lax.logistic(gate) * up).astype(BF16)
        project_out(act, wd.at[l])

    def remote(src, dst, send, recv, dev):
        return pltpu.make_async_remote_copy(src_ref=src, dst_ref=dst, send_sem=send, recv_sem=recv, device_id={"tp": dev}, device_id_type=MESH)

    def reduce_and_spread():
        pair = remote(part.at[:, other_rows], pair_in, pair_send.at[0], pair_recv.at[0], partner)
        pair.start()
        pair.wait()

        def combine(c):
            return part[c, my_rows, :].astype(F32) + pair_in[c].astype(F32)

        def scatter(step, carry):
            to = peer_chip(step)
            mine[to] = combine(to).astype(BF16)
            remote(mine.at[to], rs_in.at[chip], rs_send.at[0], rs_recv.at[0], to * 2 + core).start()
            return carry

        lax.fori_loop(1, chips, scatter, 0)
        acc = combine(chip) + hbuf[chip, my_rows, :].astype(F32)
        rest = mine.at[pl.ds(0, chips - 1)]
        whole = remote(rest, rs_in.at[pl.ds(0, chips - 1)], rs_send.at[0], rs_recv.at[0], partner)
        whole.wait_recv()

        def gather_sum(step, acc):
            return acc + rs_in[peer_chip(step)].astype(F32)

        acc = lax.fori_loop(1, chips, gather_sum, acc)
        hbuf[chip, my_rows, :] = acc.astype(BF16)
        own = hbuf.at[chip, my_rows]

        def spread(step, carry):
            remote(own, own, ag_send.at[0], ag_recv.at[chip], peer_chip(step) * 2 + core).start()
            return carry

        lax.fori_loop(1, chips, spread, 0)
        remote(own, own, fwd_send.at[0], fwd_recv.at[0], partner).start()

        def forward(step, carry):
            at = peer_chip(step)
            block = hbuf.at[at, my_rows]
            remote(block, block, ag_send.at[0], ag_recv.at[at], partner).wait_recv()
            remote(block, block, fwd_send.at[0], fwd_recv.at[0], partner).start()
            return carry

        lax.fori_loop(1, chips, forward, 0)
        whole.wait_send()
        remote(rest, rest, ag_send.at[0], rs_recv.at[0], partner).wait_send()
        remote(hbuf.at[:, my_rows], hbuf.at[:, other_rows], fwd_send.at[0], fwd_recv.at[0], partner).wait()

    for l in range(layers):
        norm(2 * l)
        attention(l)
        if l == 0:
            for later in range(1, layers):
                load_all(later)
            pl.semaphore_wait(barrier, chips)
        reduce_and_spread()
        norm(2 * l + 1)
        mlp(l)
        reduce_and_spread()

    def out_copy(c):
        return pltpu.make_async_copy(hbuf.at[c], out_hbm.at[:, pl.ds(c * LANES, LANES)], out_sem.at[c])

    for c in range(ncol):
        out_copy(c).start()
    for c in range(ncol):
        out_copy(c).wait()


def solution(mesh):
    col_spec = P(None, None, "tp")
    row_spec = P(None, "tp", None)
    cache_spec = P(None, "dp", "tp", None, None)
    in_specs = (P("dp", None), P("dp"), P(), col_spec, col_spec, col_spec, row_spec, P(), col_spec, col_spec, row_spec, cache_spec, cache_spec)
    n = mesh.shape["tp"]

    def body(x, lengths, attn_gain, w_q, w_k, w_v, w_o, mlp_gain, w_gate, w_up, w_down, k_cache, v_cache):
        tok, width = x.shape
        layers, rows, _, seq, hd = k_cache.shape
        dec, ff, chips = rows - 1, w_gate.shape[-1], n // 2
        half, ncol = tok // 2, width // LANES
        gains = jnp.stack([attn_gain, mlp_gain], axis=1)
        small = tables(lengths, tok, hd, gains)

        def flat(cache):
            return jnp.swapaxes(cache, 3, 4).reshape(layers, rows * hd, seq)

        def turned(w):
            return jnp.swapaxes(w, 1, 2)

        dma = pltpu.SemaphoreType.DMA
        vmem, hbm = pl.BlockSpec(memory_space=pltpu.VMEM), pl.BlockSpec(memory_space=pl.ANY)
        return pl.pallas_call(
            functools.partial(layers_kernel, (n, layers, tok, width, dec, seq, hd, ff)),
            out_shape=jax.ShapeDtypeStruct((tok, width), BF16),
            in_specs=[hbm] + [vmem] * 4 + [hbm] * 9,
            out_specs=hbm,
            scratch_shapes=[
                pltpu.VMEM((ncol, tok, LANES), BF16),
                pltpu.VMEM((ncol, tok, LANES), BF16),
                pltpu.VMEM((ncol, half, LANES), BF16),
                pltpu.VMEM((ncol, half, LANES), BF16),
                pltpu.VMEM((ncol, half, LANES), BF16),
                pltpu.VMEM((tok, width), BF16),
                pltpu.VMEM((tok, 3 * hd), BF16),
                pltpu.VMEM((dec, BLOCK * hd), BF16),
                pltpu.VMEM((dec, seq), F32),
                pltpu.VMEM((tok, seq), BF16),
                pltpu.VMEM((tok, hd), BF16),
                pltpu.VMEM((tok, ff), BF16),
                pltpu.VMEM((layers, 3 * hd, width), BF16),
                pltpu.VMEM((layers, hd, width), BF16),
                pltpu.VMEM((layers, width, ff), BF16),
                pltpu.VMEM((layers, width, ff), BF16),
                pltpu.VMEM((layers, ff, width), BF16),
                pltpu.VMEM((layers, rows * hd, seq), BF16),
                pltpu.VMEM((layers, rows * hd, seq), BF16),
                dma((ncol,)),
                dma((layers, 9)),
                dma((ncol,)),
                dma((1,)), dma((1,)), dma((1,)), dma((1,)), dma((1,)), dma((chips,)), dma((1,)), dma((1,)),
            ],
            compiler_params=pltpu.CompilerParams(collective_id=0, has_side_effects=True, vmem_limit_bytes=60 * 2**20),
        )(x, *small, turned(w_q), turned(w_k), turned(w_v), w_o, w_gate, w_up, w_down, flat(k_cache), flat(v_cache))

    return jax.shard_map(body, mesh=mesh, in_specs=in_specs, out_specs=P("dp", None), check_vma=False)
```

time: 454 us -> 116 us (0.26)
  waiting for transfers between devices: 381 us -> 0 us
  Pallas kernels: 0 us -> 107 us
  other arithmetic: 34.1 us -> 3.45 us
  matrix products: 20.2 us -> 0 us
  between operations: 13.5 us -> 0.04 us
    psum x4 -> x0, waiting for transfers between devices: 381 us -> none  [the longest x2 193 us: decoder_layer(): attn_sum = lax.psum(attn_part, 'tp')]
    pallas_call x0 -> x1, Pallas kernels: none -> 107 us  [body(): pl.pallas_call(functools.partial(layers_kernel, (n, layers, tok, width, d...]
    unnamed x8 -> x0, other arithmetic: 20.6 us -> none
    dot_general x20 -> x0, matrix products: 20.2 us -> none  [the longest x2 7 us: decoder_layer(): jnp.dot(activated, w_down, preferred_element_type=jnp.float32)]
    reduce_sum x8 -> x0, other arithmetic: 7.13 us -> none  [the longest x4 6.33 us: rms_norm(): jnp.mean(x_f32 * x_f32, axis=-1, keepdims=True) + EPSILON]
  transfers between devices with their start and end apart: 4 -> 0, of which waited for: 4 -> 0; matrix products, arithmetic and copies ran while one was open for 0% -> 0% of each run, Pallas kernels for 0% -> 0%
where the time goes in v1:
time: 116 us
  Pallas kernels  107 us (92%)
  local copies, waits for them, and re-layouts  5.98 us (5%)
  other arithmetic  3.45 us (3%)
    pallas_call x1, Pallas kernels, body(): pl.pallas_call(functools.partial(layers_kernel, (n, layers, tok, width, d...  107 us

profile of v1, /device:TPU:97, one launch (start us, length us, event | category | flops | bytes accessed | tf_op | source)
XLA Modules:
  0.0 116.0 jit_solution(1876020412127414659)
XLA Ops:
  0.0 1.2 %slice.9 = s32[1]{0:T(128)} slice(s32[65]{0:T(128)} %param.14), slice={[64:65]} | slice | bytes 8 | tf_op jit(solution)/shard_map/slice | solution.py:30
  1.2 1.3 %concatenate.16 = s32[72]{0:T(128)S(1)} pad(s32[64]{0:T(128)} %bitcast.20, s32[]{:T(128)} %bitcast), padding=0_8 | pad | bytes 548 | tf_op jit(solution)/shard_map/concatenate | solution.py:30
  2.5 0.6 iota_add_fusion
  3.2 0.7 add_convert_fusion
  3.9 0.7 maximum_convert_fusion
  4.7 0.6 reshape.33.gain_ref
  5.4 0.7 broadcast_in_dim.5.len_ref
  6.0 0.4 fusion
  6.5 0.9 pad_maximum_fusion
  7.4 106.5 %shard_map.127 = bf16[192,2048]{1,0:T(8,128)(2,1)} custom-call(bf16[192,2048]{1,0:T(8,128)(2,1)} %x_hbm.1, s32[72,128]{1,0:T(8,128)} %broadcast_in_dim.5.len_ref, f32[192,128]{1,0:T(8,128)} %get-tuple-element.8.cos_ref, f32[192,128]{1,0:T(8,128)} %get-tuple-element.9.sin_ref, f32[64,128]{1,0:T(8,128)} %reshape.33.gain_ref, bf16[2,64,2048]{2,1,0:T(8,128)(2,1)} %bitcast.15, ...), custom_call_target="tpu_custom_call" | custom-call | tf_op jit(solution)/shard_map/pallas_call | solution.py:291
  113.9 2.1 %copy.16 = bf16[192,2048]{1,0:T(8,128)(2,1)} copy(bf16[192,2048]{1,0:T(8,128)(2,1)} %shard_map.127) | data formatting | bytes 1572864
  (2 shorter events, 0.0 us)

commit v2 on v1

v2 whole, which is shorter than its diff:
```python
import functools

import jax
import jax.numpy as jnp
from jax import lax
from jax.experimental import pallas as pl
from jax.experimental.pallas import tpu as pltpu
from jax.sharding import PartitionSpec as P

ROPE_BASE = 500000.0
EPSILON = 1e-5
MESH = pl.DeviceIdType.MESH
LANES = 128
SUBLANES = 8
BLOCK = 16
F32 = jnp.float32
BF16 = jnp.bfloat16


def nt_dot(a, b):
    return lax.dot_general(a, b, (((1,), (1,)), ((), ())), preferred_element_type=F32)


def layers_kernel(dims, len_ref, again_ref, mgain_ref, x_hbm, wq_hbm, wk_hbm, wv_hbm, wo_hbm, wg_hbm, wu_hbm, wd_hbm, kc_hbm, vc_hbm, out_ref,
                  hbuf, part, pair_in, mine, rs_in, normed, qkv, qbd, logits, probs, attended, act, cos_ref, sin_ref, len_col, gains,
                  wqkv, wo, wg, wu, wd, kc, vc,
                  x_sem, w_sem, pair_send, pair_recv, rs_send, rs_recv, ag_send, ag_recv, fwd_send, fwd_recv):
    n, layers, tok, width, dec, seq, hd, ff = dims
    chips = n // 2
    side = int(round(chips ** 0.5))
    chunk = tok - dec
    ncol = width // LANES
    ngrp = ncol // 2
    me = lax.axis_index("tp")
    core = lax.rem(me, 2)
    chip = me // 2
    my_y, my_x = chip // side, lax.rem(chip, side)
    partner = chip * 2 + (1 - core)
    my_base, other_base = core * ngrp, (1 - core) * ngrp
    streams = ((0, dec), (dec, chunk))
    DEC, PRE = 0, 1

    def peer_chip(step):
        return lax.rem(my_y + step // side, side) * side + lax.rem(my_x + lax.rem(step, side), side)

    barrier = pltpu.get_barrier_semaphore()
    pl.semaphore_signal(barrier, inc=1, device_id={"tp": partner}, device_id_type=MESH)

    def greet(step, carry):
        pl.semaphore_signal(barrier, inc=1, device_id={"tp": peer_chip(step) * 2 + core}, device_id_type=MESH)
        return carry

    lax.fori_loop(1, chips, greet, 0)

    def x_copy(c):
        return pltpu.make_async_copy(x_hbm.at[:, pl.ds(c * LANES, LANES)], hbuf.at[c], x_sem.at[c])

    def load(l, name):
        if name == "pre_keys":
            return pltpu.make_async_copy(kc_hbm.at[l, pl.ds(dec * hd, hd)], kc.at[l, pl.ds(dec * hd, hd)], w_sem.at[l, 9])
        if name == "pre_values":
            return pltpu.make_async_copy(vc_hbm.at[l, pl.ds(dec * hd, hd)], vc.at[l, pl.ds(dec * hd, hd)], w_sem.at[l, 10])
        i, src, dst = {
            "q": (0, wq_hbm.at[l], wqkv.at[l, pl.ds(0, hd)]),
            "k": (1, wk_hbm.at[l], wqkv.at[l, pl.ds(hd, hd)]),
            "v": (2, wv_hbm.at[l], wqkv.at[l, pl.ds(2 * hd, hd)]),
            "o": (3, wo_hbm.at[l], wo.at[l]),
            "gate": (4, wg_hbm.at[l], wg.at[l]),
            "up": (5, wu_hbm.at[l], wu.at[l]),
            "down": (6, wd_hbm.at[l], wd.at[l]),
            "keys": (7, kc_hbm.at[l, pl.ds(0, dec * hd)], kc.at[l, pl.ds(0, dec * hd)]),
            "values": (8, vc_hbm.at[l, pl.ds(0, dec * hd)], vc.at[l, pl.ds(0, dec * hd)]),
        }[name]
        return pltpu.make_async_copy(src, dst, w_sem.at[l, i])

    def load_all(l):
        for name in ("q", "k", "v", "pre_keys", "pre_values", "o", "keys", "values", "gate", "up", "down"):
            load(l, name).start()

    for c in range(ncol):
        x_copy(c).start()
    load_all(0)

    row8 = lax.broadcasted_iota(jnp.int32, (SUBLANES, LANES), 0)
    for b in range(dec // SUBLANES):
        col = jnp.zeros((SUBLANES, LANES), jnp.int32)
        for i in range(SUBLANES):
            col = jnp.where(row8 == i, len_ref[b * SUBLANES + i], col)
        len_col[b * SUBLANES:(b + 1) * SUBLANES, :] = col
    prefix = len_ref[dec]
    lane_f = lax.broadcasted_iota(jnp.int32, (1, LANES), 1)
    freq_exps = (2 * lax.rem(lane_f, hd // 2)).astype(F32) / hd
    freqs = jnp.exp(-freq_exps * jnp.log(jnp.full((1, LANES), ROPE_BASE, F32)))
    sign = jnp.where(lax.rem(lane_f, hd) < hd // 2, -1.0, 1.0)
    pos = jnp.concatenate([len_col[...], prefix + lax.broadcasted_iota(jnp.int32, (chunk, LANES), 0)], axis=0)
    angles = pos.astype(F32) * freqs
    cos_ref[...] = jnp.cos(angles)
    sin_ref[...] = jnp.sin(angles) * sign
    gains[0:layers, :] = again_ref[...].astype(F32)
    gains[layers:, :] = mgain_ref[...].astype(F32)

    for c in range(ncol):
        x_copy(c).wait()

    def norm(s, gain_row):
        r0, rows = streams[s]
        total = jnp.zeros((rows, LANES), F32)
        for c in range(ncol):
            h = hbuf[c, r0:r0 + rows, :].astype(F32)
            total += h * h
        inv = lax.rsqrt(jnp.sum(total, axis=1, keepdims=True) / width + EPSILON)
        for c in range(ncol):
            gain = gains[gain_row:gain_row + 1, c * LANES:(c + 1) * LANES]
            normed[r0:r0 + rows, c * LANES:(c + 1) * LANES] = (hbuf[c, r0:r0 + rows, :].astype(F32) * inv * gain).astype(BF16)

    def project_qkv(s, l):
        r0, rows = streams[s]
        proj = nt_dot(normed[r0:r0 + rows, :], wqkv[l]).astype(BF16)
        lane = lax.broadcasted_iota(jnp.int32, (rows, LANES), 1)
        qk = proj[:, :2 * hd].astype(F32)
        turned = jnp.where(lax.rem(lane, hd) < hd // 2, pltpu.roll(qk, LANES - hd // 2, 1), pltpu.roll(qk, hd // 2, 1))
        qk = (qk * cos_ref[r0:r0 + rows, :] + turned * sin_ref[r0:r0 + rows, :]).astype(BF16)
        qkv[r0:r0 + rows, :2 * hd] = qk
        qkv[r0:r0 + rows, 2 * hd:3 * hd] = proj[:, 2 * hd:]

    scale = hd ** -0.5

    def decode_attention(l):
        lane = lax.broadcasted_iota(jnp.int32, (dec, LANES), 1)
        qk = qkv[0:dec, :2 * hd].astype(F32)
        swapped = pltpu.roll(qk, hd, 1)
        q_twice = jnp.where(lane < hd, qk, swapped)
        k_twice = jnp.where(lane < hd, swapped, qk)
        row = lax.rem(lax.broadcasted_iota(jnp.int32, (dec, LANES), 0), BLOCK)
        for j in range(BLOCK * hd // LANES):
            qbd[:, j * LANES:(j + 1) * LANES] = jnp.where(row == 2 * j + lane // hd, q_twice, 0.0).astype(BF16)
        self_logit = jnp.sum(jnp.where(lane < hd, q_twice * k_twice, 0.0), axis=1, keepdims=True) * scale
        span = BLOCK * hd

        def dec_logits(g, carry):
            rows = pl.ds(pl.multiple_of(g * BLOCK, BLOCK), BLOCK)
            keys = kc[l, pl.ds(pl.multiple_of(g * span, span), span), :]
            logits[rows, :] = jnp.dot(qbd[rows, :], keys, preferred_element_type=F32)
            return carry

        lax.fori_loop(0, dec // BLOCK, dec_logits, 0)
        pos = lax.broadcasted_iota(jnp.int32, (dec, seq), 1)
        lg = jnp.where(pos < len_col[:, 0:1], logits[0:dec, :] * scale, -jnp.inf)
        top = jnp.maximum(jnp.max(lg, axis=1, keepdims=True), self_logit)
        ex = jnp.exp(lg - top)
        ex_self = jnp.exp(self_logit - top)
        inv = 1.0 / (jnp.sum(ex, axis=1, keepdims=True) + ex_self)
        probs[0:dec, :] = (ex * inv).astype(BF16)
        p_self = (ex_self * inv).astype(BF16).astype(F32)
        lane_b = lax.broadcasted_iota(jnp.int32, (BLOCK, LANES), 1)
        row_b = lax.broadcasted_iota(jnp.int32, (BLOCK, LANES), 0)

        def dec_values(g, carry):
            rows = pl.ds(pl.multiple_of(g * BLOCK, BLOCK), BLOCK)
            full = nt_dot(probs[rows, :], vc[l, pl.ds(pl.multiple_of(g * span, span), span), :])
            acc = jnp.zeros((BLOCK, LANES), F32)
            for j in range(BLOCK * hd // LANES):
                acc += jnp.where(row_b == 2 * j + lane_b // hd, full[:, j * LANES:(j + 1) * LANES], 0.0)
            logits[rows, 0:LANES] = acc + pltpu.roll(acc, hd, 1)
            return carry

        lax.fori_loop(0, dec // BLOCK, dec_values, 0)
        attended[0:dec, :] = (logits[0:dec, 0:hd] + p_self * qkv[0:dec, 2 * hd:3 * hd].astype(F32)).astype(BF16)

    def prefill_attention(l):
        q_chk = qkv[dec:, 0:hd]
        lg = jnp.dot(q_chk, kc[l, dec * hd:(dec + 1) * hd, :], preferred_element_type=F32) * scale
        lg_new = nt_dot(q_chk, qkv[dec:, hd:2 * hd]) * scale
        pos = lax.broadcasted_iota(jnp.int32, (chunk, seq), 1)
        lg = jnp.where(pos < prefix, lg, -jnp.inf)
        tok_r = lax.broadcasted_iota(jnp.int32, (chunk, chunk), 0)
        tok_c = lax.broadcasted_iota(jnp.int32, (chunk, chunk), 1)
        lg_new = jnp.where(tok_c <= tok_r, lg_new, -jnp.inf)
        top = jnp.maximum(jnp.max(lg, axis=1, keepdims=True), jnp.max(lg_new, axis=1, keepdims=True))
        ex, ex_new = jnp.exp(lg - top), jnp.exp(lg_new - top)
        inv = 1.0 / (jnp.sum(ex, axis=1, keepdims=True) + jnp.sum(ex_new, axis=1, keepdims=True))
        p_old = (ex * inv).astype(BF16)
        p_new = (ex_new * inv).astype(BF16)
        out = nt_dot(p_old, vc[l, dec * hd:(dec + 1) * hd, :])
        out += jnp.dot(p_new, qkv[dec:, 2 * hd:3 * hd], preferred_element_type=F32)
        attended[dec:, :] = out.astype(BF16)

    def remote(src, dst, send, recv, dev):
        return pltpu.make_async_remote_copy(src_ref=src, dst_ref=dst, send_sem=send, recv_sem=recv, device_id={"tp": dev}, device_id_type=MESH)

    def pair_copy(s):
        r0, rows = streams[s]
        return remote(part.at[pl.ds(other_base, ngrp), pl.ds(r0, rows)], pair_in.at[:, pl.ds(r0, rows)], pair_send.at[s], pair_recv.at[s], partner)

    def project_out(s, lhs_ref, w_ref):
        r0, rows = streams[s]
        lhs = lhs_ref[r0:r0 + rows, :]
        step = min(4, ngrp)
        for base in (other_base, my_base):
            for c in range(0, ngrp, step):
                at = pl.multiple_of((base + c) * LANES, LANES)
                out = jnp.dot(lhs, w_ref[:, pl.ds(at, step * LANES)], preferred_element_type=F32).astype(BF16)
                for j in range(step):
                    part[base + c + j, r0:r0 + rows, :] = out[:, j * LANES:(j + 1) * LANES]
            if base is other_base:
                pair_copy(s).start()

    def block_at(s, c):
        r0, rows = streams[s]
        half = rows // 2
        return lax.rem(c, ngrp), pl.ds(pl.multiple_of(r0 + (c // ngrp) * half, half), half)

    def own_rows(s):
        r0, rows = streams[s]
        return pl.ds(r0 // 2, rows // 2)

    def start_compute(s, phase):
        l = phase // 2
        r0, rows = streams[s]
        norm(s, l + layers * (phase % 2))
        if phase % 2 == 0:
            if s == PRE:
                for name in ("q", "k", "v"):
                    load(l, name).wait()
            project_qkv(s, l)
        else:
            if s == PRE:
                load(l, "gate").wait()
                load(l, "up").wait()
            a = normed[r0:r0 + rows, :]
            gate = jnp.dot(a, wg[l], preferred_element_type=F32)
            up = jnp.dot(a, wu[l], preferred_element_type=F32)
            act[r0:r0 + rows, :] = (gate * lax.logistic(gate) * up).astype(BF16)

    def end_compute(s, phase):
        l = phase // 2
        if phase % 2 == 0:
            if s == PRE:
                load(l, "pre_keys").wait()
                load(l, "pre_values").wait()
                prefill_attention(l)
                load(l, "o").wait()
            else:
                load(l, "keys").wait()
                load(l, "values").wait()
                decode_attention(l)
            if phase == 0 and s == PRE:
                pl.semaphore_wait(barrier, chips)
            project_out(s, attended, wo.at[l])
        else:
            if s == PRE:
                load(l, "down").wait()
            project_out(s, act, wd.at[l])

    def combine(s, c):
        group, rows = block_at(s, c)
        return part[my_base + group, rows, :].astype(F32) + pair_in[group, rows, :].astype(F32)

    def scatter(s):
        pair_copy(s).wait()
        slot = own_rows(s)

        def send(step, carry):
            to = peer_chip(step)
            mine[to, slot, :] = combine(s, to).astype(BF16)
            remote(mine.at[to, slot], rs_in.at[chip, slot], rs_send.at[s], rs_recv.at[s], to * 2 + core).start()
            return carry

        lax.fori_loop(1, chips, send, 0)

    def scattered(s):
        blocks = pl.ds(0, chips - 1)
        return remote(mine.at[blocks, own_rows(s)], rs_in.at[blocks, own_rows(s)], rs_send.at[s], rs_recv.at[s], partner)

    def spread(s):
        group, rows = block_at(s, chip)
        own = hbuf.at[my_base + group, rows]
        acc = combine(s, chip) + hbuf[my_base + group, rows, :].astype(F32)
        scattered(s).wait_recv()

        def add(step, acc):
            return acc + rs_in[peer_chip(step), own_rows(s), :].astype(F32)

        hbuf[my_base + group, rows, :] = lax.fori_loop(1, chips, add, acc).astype(BF16)

        def send(step, carry):
            remote(own, own, ag_send.at[s], ag_recv.at[s, chip], peer_chip(step) * 2 + core).start()
            return carry

        lax.fori_loop(1, chips, send, 0)
        remote(own, own, fwd_send.at[s], fwd_recv.at[s], partner).start()

    def forward(s):
        def hand_on(step, carry):
            at = peer_chip(step)
            group, rows = block_at(s, at)
            block = hbuf.at[my_base + group, rows]
            remote(block, block, ag_send.at[s], ag_recv.at[s, at], partner).wait_recv()
            remote(block, block, fwd_send.at[s], fwd_recv.at[s], partner).start()
            return carry

        lax.fori_loop(1, chips, hand_on, 0)

    def finish(s):
        r0, rows = streams[s]
        blocks = pl.ds(0, chips - 1)
        scattered(s).wait_send()
        remote(mine.at[blocks, own_rows(s)], rs_in.at[blocks, own_rows(s)], ag_send.at[s], rs_recv.at[s], partner).wait_send()
        remote(hbuf.at[pl.ds(my_base, ngrp), pl.ds(r0, rows)], hbuf.at[pl.ds(other_base, ngrp), pl.ds(r0, rows)], fwd_send.at[s], fwd_recv.at[s], partner).wait()

    phases = 2 * layers
    start_compute(PRE, 0)
    end_compute(PRE, 0)
    for phase in range(phases):
        if phase > 0:
            forward(DEC)
            scatter(PRE)
            finish(DEC)
            start_compute(DEC, phase)
        else:
            start_compute(DEC, phase)
            scatter(PRE)
            for later in range(1, layers):
                load_all(later)
        end_compute(DEC, phase)
        scatter(DEC)
        spread(PRE)
        spread(DEC)
        forward(PRE)
        finish(PRE)
        if phase + 1 < phases:
            start_compute(PRE, phase + 1)
            end_compute(PRE, phase + 1)
    r0, rows = streams[PRE]
    for c in range(ncol):
        out_ref[r0:r0 + rows, c * LANES:(c + 1) * LANES] = hbuf[c, r0:r0 + rows, :]
    forward(DEC)
    finish(DEC)
    r0, rows = streams[DEC]
    for c in range(ncol):
        out_ref[r0:r0 + rows, c * LANES:(c + 1) * LANES] = hbuf[c, r0:r0 + rows, :]


def solution(mesh):
    col_spec = P(None, None, "tp")
    row_spec = P(None, "tp", None)
    cache_spec = P(None, "dp", "tp", None, None)
    in_specs = (P("dp", None), P("dp"), P(), col_spec, col_spec, col_spec, row_spec, P(), col_spec, col_spec, row_spec, cache_spec, cache_spec)
    n = mesh.shape["tp"]

    def body(x, lengths, attn_gain, w_q, w_k, w_v, w_o, mlp_gain, w_gate, w_up, w_down, k_cache, v_cache):
        tok, width = x.shape
        layers, rows, _, seq, hd = k_cache.shape
        dec, ff, chips = rows - 1, w_gate.shape[-1], n // 2
        half, ncol = tok // 2, width // LANES

        def flat(cache):
            return jnp.swapaxes(cache, 3, 4).reshape(layers, rows * hd, seq)

        def turned(w):
            return jnp.swapaxes(w, 1, 2)

        dma = pltpu.SemaphoreType.DMA
        vmem, hbm, smem = (pl.BlockSpec(memory_space=m) for m in (pltpu.VMEM, pltpu.HBM, pltpu.SMEM))
        return pl.pallas_call(
            functools.partial(layers_kernel, (n, layers, tok, width, dec, seq, hd, ff)),
            out_shape=jax.ShapeDtypeStruct((tok, width), BF16),
            in_specs=[smem, vmem, vmem] + [hbm] * 10,
            out_specs=vmem,
            scratch_shapes=[
                pltpu.VMEM((ncol, tok, LANES), BF16),
                pltpu.VMEM((ncol, tok, LANES), BF16),
                pltpu.VMEM((ncol // 2, tok, LANES), BF16),
                pltpu.VMEM((chips, half, LANES), BF16),
                pltpu.VMEM((chips, half, LANES), BF16),
                pltpu.VMEM((tok, width), BF16),
                pltpu.VMEM((tok, 3 * hd), BF16),
                pltpu.VMEM((dec, BLOCK * hd), BF16),
                pltpu.VMEM((dec, seq), F32),
                pltpu.VMEM((dec, seq), BF16),
                pltpu.VMEM((tok, hd), BF16),
                pltpu.VMEM((tok, ff), BF16),
                pltpu.VMEM((tok, LANES), F32),
                pltpu.VMEM((tok, LANES), F32),
                pltpu.VMEM((dec, LANES), jnp.int32),
                pltpu.VMEM((2 * layers, width), F32),
                pltpu.VMEM((layers, 3 * hd, width), BF16),
                pltpu.VMEM((layers, hd, width), BF16),
                pltpu.VMEM((layers, width, ff), BF16),
                pltpu.VMEM((layers, width, ff), BF16),
                pltpu.VMEM((layers, ff, width), BF16),
                pltpu.VMEM((layers, rows * hd, seq), BF16),
                pltpu.VMEM((layers, rows * hd, seq), BF16),
                dma((ncol,)),
                dma((layers, 11)),
                dma((2,)), dma((2,)), dma((2,)), dma((2,)), dma((2,)), dma((2, chips)), dma((2,)), dma((2,)),
            ],
            compiler_params=pltpu.CompilerParams(collective_id=0, has_side_effects=True, vmem_limit_bytes=63 * 2**20),
        )(lengths, attn_gain, mlp_gain, x, turned(w_q), turned(w_k), turned(w_v), w_o, w_gate, w_up, w_down, flat(k_cache), flat(v_cache))

    return jax.shard_map(body, mesh=mesh, in_specs=in_specs, out_specs=P("dp", None), check_vma=False)
```

time: 116 us -> 91.4 us (0.79)
  Pallas kernels: 107 us -> 89.1 us
  local copies, waits for them, and re-layouts: 5.98 us -> 2.09 us
  other arithmetic: 3.45 us -> 0 us
    pallas_call x1, Pallas kernels: 107 us -> 89.1 us  [body(): pl.pallas_call(functools.partial(layers_kernel, (n, layers, tok, width, d...]
    convert_element_type x2 -> x0, other arithmetic: 1.48 us -> none  [the longest x1 0.75 us: tables(): return (len_tab, cos_tab, sin_tab, gains.astype(F32).reshape(-1, LANES))]
    concatenate x1 -> x0, local copies, waits for them, and re-layouts: 1.3 us -> none  [tables(): jnp.concatenate([lengths[:dec], jnp.broadcast_to(lengths[dec:], (8,))])]
    slice x1 -> x0, local copies, waits for them, and re-layouts: 1.24 us -> none  [tables(): lengths[dec:]]
where the time goes in v2:
time: 91.4 us; the launch traced here: 91.2 us
  Pallas kernels  89.1 us (97%)
  local copies, waits for them, and re-layouts  2.09 us (2%)
    pallas_call x1, Pallas kernels, body(): pl.pallas_call(functools.partial(layers_kernel, (n, layers, tok, width, d...  89.1 us
    unnamed x1, local copies, waits for them, and re-layouts  2.09 us

profile of v2, /device:TPU:97, one launch (start us, length us, event | category | flops | bytes accessed | tf_op | source)
XLA Modules:
  0.0 91.2 jit_solution(128649017154102155)
XLA Ops:
  0.0 89.1 %shard_map.127 = bf16[192,2048]{1,0:T(8,128)(2,1)} custom-call(s32[65]{0:T(128)} %len_ref.1, bf16[2,2048]{1,0:T(2,128)(2,1)} %again_ref.1, bf16[2,2048]{1,0:T(2,128)(2,1)} %mgain_ref.1, bf16[192,2048]{1,0:T(8,128)(2,1)} %x_hbm.1, bf16[2,64,2048]{2,1,0:T(8,128)(2,1)} %bitcast.11, bf16[2,64,2048]{2,1,0:T(8,128)(2,1)} %bitcast.12, ...), custom_call_target="tpu_custom_call" | custom-call | tf_op jit(solution)/shard_map/pallas_call | solution.py:365
  89.1 2.1 %copy.15 = bf16[192,2048]{1,0:T(8,128)(2,1)} copy(bf16[192,2048]{1,0:T(8,128)(2,1)} %shard_map.127) | data formatting | bytes 1572864

commit v3 on v2

v3 whole, which is shorter than its diff:
```python
import functools

import jax
import jax.numpy as jnp
from jax import lax
from jax.experimental import pallas as pl
from jax.experimental.pallas import tpu as pltpu
from jax.sharding import PartitionSpec as P

ROPE_BASE = 500000.0
EPSILON = 1e-5
MESH = pl.DeviceIdType.MESH
LANES = 128
SUBLANES = 8
BLOCK = 16
DECODE_STREAMS, PREFILL_STREAMS = 2, 2
ORDER = (3, 0, 0, 1, 2, 0, 3, 0, 2, 3, 1, 2, 1, 0, 1, 3, 2, 0, 0, 0, 0, 3, 0, 2, 3, 1, 3, 3, 2, 2, 2, 3, 2, 0, 1, 1, 1, 3, 1, 2, 0, 1, 0, 0, 0, 0, 3, 2, 1, 0, 3, 3, 2, 2, 3, 2, 3, 1, 0, 2, 1, 1, 1, 1, 3, 1, 2, 0, 0, 3, 1, 2, 3, 0, 3, 3, 2, 0, 2, 3, 2, 1, 2, 1, 1, 1, 0, 1, 3, 2, 0, 1, 2, 0, 3, 1, 3, 2, 0, 1)
MIB = 2**20
PIECE = MIB // 2
PACE = {"start": 2 * MIB, "middle": 4 * MIB, "end": 2 * MIB, "scatter": MIB // 2, "spread": MIB // 2, "forward": 0, "finish": 0}
F32 = jnp.float32
BF16 = jnp.bfloat16


def nt_dot(a, b):
    return lax.dot_general(a, b, (((1,), (1,)), ((), ())), preferred_element_type=F32)


def split_rows(dec, chunk):
    d, c = dec // DECODE_STREAMS, chunk // PREFILL_STREAMS
    rows = [(i * d, d) for i in range(DECODE_STREAMS)] + [(dec + i * c, c) for i in range(PREFILL_STREAMS)]
    return tuple(rows), DECODE_STREAMS


def stage_order(streams, decode_streams, phases):
    chains = []
    for s in range(len(streams)):
        chain = []
        for phase in range(phases):
            middle = ["middle"] if s < decode_streams and phase % 2 == 0 else []
            chain += [(s, name, phase) for name in ["start"] + middle + ["end", "scatter", "spread", "forward", "finish"]]
        chains.append(iter(chain))
    return [next(chains[s]) for s in ORDER]


def layers_kernel(dims, len_ref, again_ref, mgain_ref, x_hbm, wq_hbm, wk_hbm, wv_hbm, wo_hbm, wg_hbm, wu_hbm, wd_hbm, kc_hbm, vc_hbm, out_ref,
                  hbuf, part, pair_in, mine, rs_in, normed, qkv, qbd, logits, probs, v_self, attended, act, cos_ref, sin_ref, len_col, gains,
                  wqkv, wo, wg, wu, wd, kc, vc,
                  x_sem, w_sem, pair_send, pair_recv, rs_send, rs_recv, ag_send, ag_recv, fwd_send, fwd_recv):
    n, layers, tok, width, dec, seq, hd, ff = dims
    chips = n // 2
    side = int(round(chips ** 0.5))
    chunk = tok - dec
    ncol = width // LANES
    ngrp = ncol // 2
    me = lax.axis_index("tp")
    core = lax.rem(me, 2)
    chip = me // 2
    my_y, my_x = chip // side, lax.rem(chip, side)
    partner = chip * 2 + (1 - core)
    my_base, other_base = core * ngrp, (1 - core) * ngrp
    streams, decode_streams = split_rows(dec, chunk)

    def hops(step):
        return sum(min(d, side - d) for d in divmod(step, side))

    peers = []
    for step in sorted(range(1, chips), key=lambda step: -hops(step)):
        at = lax.rem(my_y + step // side, side) * side + lax.rem(my_x + step % side, side)
        peers.append((at, at * 2 + core, lax.rem(at, ngrp), at // ngrp))

    barrier = pltpu.get_barrier_semaphore()
    pl.semaphore_signal(barrier, inc=1, device_id={"tp": partner}, device_id_type=MESH)

    for _, device, _, _ in peers:
        pl.semaphore_signal(barrier, inc=1, device_id={"tp": device}, device_id_type=MESH)

    def x_copy(c):
        return pltpu.make_async_copy(x_hbm.at[:, pl.ds(c * LANES, LANES)], hbuf.at[c], x_sem.at[c])

    def parts_of(l, name):
        def cache(src, dst, first, rows, i):
            at = pl.ds(first * hd, rows * hd)
            return src.at[l, at], dst.at[l, at], w_sem.at[l, i], rows * hd

        if name[:4] in ("keys", "valu"):
            s = int(name[-1])
            src, dst, i = (kc_hbm, kc, 9 + 2 * s) if name[0] == "k" else (vc_hbm, vc, 10 + 2 * s)
            return cache(src, dst, *streams[s], i)
        return {
            "q": lambda: (wq_hbm.at[l], wqkv.at[l, pl.ds(0, hd)], w_sem.at[l, 0], hd),
            "k": lambda: (wk_hbm.at[l], wqkv.at[l, pl.ds(hd, hd)], w_sem.at[l, 1], hd),
            "v": lambda: (wv_hbm.at[l], wqkv.at[l, pl.ds(2 * hd, hd)], w_sem.at[l, 2], hd),
            "o": lambda: (wo_hbm.at[l], wo.at[l], w_sem.at[l, 3], hd),
            "gate": lambda: (wg_hbm.at[l], wg.at[l], w_sem.at[l, 4], width),
            "up": lambda: (wu_hbm.at[l], wu.at[l], w_sem.at[l, 5], width),
            "down": lambda: (wd_hbm.at[l], wd.at[l], w_sem.at[l, 6], ff),
            "pre_keys": lambda: cache(kc_hbm, kc, dec, 1, 7),
            "pre_values": lambda: cache(vc_hbm, vc, dec, 1, 8),
        }[name]()

    def load(l, name):
        src, dst, sem, _ = parts_of(l, name)
        return pltpu.make_async_copy(src, dst, sem)

    early = ("q", "k", "v", "pre_keys", "pre_values")
    late = [f"{kind}{s}" for s in range(decode_streams) for kind in ("keys", "values")] + ["o", "gate", "up", "down"]
    pending = []
    for l in range(1, layers):
        for name in (*early, "o", *late[:-4], "gate", "up", "down"):
            src, dst, sem, rows = parts_of(l, name)
            piece = min(rows, PIECE // (2 * src.shape[-1]))
            pending += [(src.at[pl.ds(at, piece)], dst.at[pl.ds(at, piece)], sem, piece * src.shape[-1] * 2) for at in range(0, rows, piece)]

    def prefetch(budget):
        while pending and budget > 0:
            src, dst, sem, size = pending.pop(0)
            pltpu.make_async_copy(src, dst, sem).start()
            budget -= size

    for c in range(ncol):
        x_copy(c).start()
    for name in early:
        load(0, name).start()

    row8 = lax.broadcasted_iota(jnp.int32, (SUBLANES, LANES), 0)
    for b in range(dec // SUBLANES):
        col = jnp.zeros((SUBLANES, LANES), jnp.int32)
        for i in range(SUBLANES):
            col = jnp.where(row8 == i, len_ref[b * SUBLANES + i], col)
        len_col[b * SUBLANES:(b + 1) * SUBLANES, :] = col
    prefix = len_ref[dec]
    lane_f = lax.broadcasted_iota(jnp.int32, (1, LANES), 1)
    freq_exps = (2 * lax.rem(lane_f, hd // 2)).astype(F32) / hd
    freqs = jnp.exp(-freq_exps * jnp.log(jnp.full((1, LANES), ROPE_BASE, F32)))
    sign = jnp.where(lax.rem(lane_f, hd) < hd // 2, -1.0, 1.0)
    pos = jnp.concatenate([len_col[...], prefix + lax.broadcasted_iota(jnp.int32, (chunk, LANES), 0)], axis=0)
    angles = pos.astype(F32) * freqs
    cos_ref[...] = jnp.cos(angles)
    sin_ref[...] = jnp.sin(angles) * sign
    for first, ref in ((0, again_ref), (layers, mgain_ref)):
        gain = ref[...].astype(F32)
        for l in range(layers):
            for c in range(ncol):
                gains[first + l, c] = gain[l:l + 1, c * LANES:(c + 1) * LANES]

    for c in range(ncol):
        x_copy(c).wait()
    for name in late:
        load(0, name).start()

    def norm(s, gain_row):
        r0, rows = streams[s]
        h = hbuf[:, r0:r0 + rows, :].astype(F32)
        total = jnp.sum(jnp.sum(h * h, axis=0), axis=1, keepdims=True)
        inv = lax.rsqrt(total / width + EPSILON)
        h = (hbuf[:, r0:r0 + rows, :].astype(F32) * inv[None] * gains[gain_row]).astype(BF16)
        for c in range(ncol):
            normed[r0:r0 + rows, c * LANES:(c + 1) * LANES] = h[c]

    def project_qkv(s, l):
        r0, rows = streams[s]
        proj = nt_dot(normed[r0:r0 + rows, :], wqkv[l]).astype(BF16)
        lane = lax.broadcasted_iota(jnp.int32, (rows, LANES), 1)
        qk = proj[:, :2 * hd].astype(F32)
        turned = jnp.where(lax.rem(lane, hd) < hd // 2, pltpu.roll(qk, LANES - hd // 2, 1), pltpu.roll(qk, hd // 2, 1))
        qk = (qk * cos_ref[r0:r0 + rows, :] + turned * sin_ref[r0:r0 + rows, :]).astype(BF16)
        qkv[r0:r0 + rows, :2 * hd] = qk
        qkv[r0:r0 + rows, 2 * hd:3 * hd] = proj[:, 2 * hd:]

    scale = hd ** -0.5

    def decode_logits(s, l):
        r0, rows = streams[s]
        lane = lax.broadcasted_iota(jnp.int32, (rows, LANES), 1)
        qk = qkv[r0:r0 + rows, :2 * hd].astype(F32)
        swapped = pltpu.roll(qk, hd, 1)
        q_twice = jnp.where(lane < hd, qk, swapped)
        k_twice = jnp.where(lane < hd, swapped, qk)
        row = lax.rem(lax.broadcasted_iota(jnp.int32, (rows, LANES), 0), BLOCK)
        for j in range(BLOCK * hd // LANES):
            qbd[r0:r0 + rows, j * LANES:(j + 1) * LANES] = jnp.where(row == 2 * j + lane // hd, q_twice, 0.0).astype(BF16)
        self_logit = jnp.sum(jnp.where(lane < hd, q_twice * k_twice, 0.0), axis=1, keepdims=True) * scale
        need(l, f"keys{s}")
        span = BLOCK * hd
        for g in range(r0 // BLOCK, (r0 + rows) // BLOCK):
            at = slice(g * BLOCK, (g + 1) * BLOCK)
            logits[at, :] = jnp.dot(qbd[at, :], kc[l, g * span:(g + 1) * span, :], preferred_element_type=F32)
        pos = lax.broadcasted_iota(jnp.int32, (rows, seq), 1)
        lg = jnp.where(pos < len_col[r0:r0 + rows, 0:1], logits[r0:r0 + rows, :] * scale, -jnp.inf)
        top = jnp.maximum(jnp.max(lg, axis=1, keepdims=True), self_logit)
        ex = jnp.exp(lg - top)
        ex_self = jnp.exp(self_logit - top)
        inv = 1.0 / (jnp.sum(ex, axis=1, keepdims=True) + ex_self)
        probs[r0:r0 + rows, :] = (ex * inv).astype(BF16)
        p_self = (ex_self * inv).astype(BF16).astype(F32)
        v_self[r0:r0 + rows, :] = p_self * qkv[r0:r0 + rows, 2 * hd:3 * hd].astype(F32)

    def decode_values(s, l):
        need(l, f"values{s}")
        r0, rows = streams[s]
        span = BLOCK * hd
        lane_b = lax.broadcasted_iota(jnp.int32, (BLOCK, LANES), 1)
        row_b = lax.broadcasted_iota(jnp.int32, (BLOCK, LANES), 0)

        for g in range(r0 // BLOCK, (r0 + rows) // BLOCK):
            at = slice(g * BLOCK, (g + 1) * BLOCK)
            full = nt_dot(probs[at, :], vc[l, g * span:(g + 1) * span, :])
            acc = jnp.zeros((BLOCK, LANES), F32)
            for j in range(BLOCK * hd // LANES):
                acc += jnp.where(row_b == 2 * j + lane_b // hd, full[:, j * LANES:(j + 1) * LANES], 0.0)
            acc += pltpu.roll(acc, hd, 1)
            attended[at, :] = (acc[:, 0:hd] + v_self[at, :]).astype(BF16)

    def prefill_attention(s, l):
        r0, rows = streams[s]
        seen = r0 + rows - dec
        q_chk = qkv[r0:r0 + rows, 0:hd]
        lg = jnp.dot(q_chk, kc[l, dec * hd:(dec + 1) * hd, :], preferred_element_type=F32) * scale
        lg_new = nt_dot(q_chk, qkv[dec:dec + seen, hd:2 * hd]) * scale
        pos = lax.broadcasted_iota(jnp.int32, (rows, seq), 1)
        lg = jnp.where(pos < prefix, lg, -jnp.inf)
        tok_r = lax.broadcasted_iota(jnp.int32, (rows, seen), 0) + (r0 - dec)
        tok_c = lax.broadcasted_iota(jnp.int32, (rows, seen), 1)
        lg_new = jnp.where(tok_c <= tok_r, lg_new, -jnp.inf)
        top = jnp.maximum(jnp.max(lg, axis=1, keepdims=True), jnp.max(lg_new, axis=1, keepdims=True))
        ex, ex_new = jnp.exp(lg - top), jnp.exp(lg_new - top)
        inv = 1.0 / (jnp.sum(ex, axis=1, keepdims=True) + jnp.sum(ex_new, axis=1, keepdims=True))
        p_old = (ex * inv).astype(BF16)
        p_new = (ex_new * inv).astype(BF16)
        out = nt_dot(p_old, vc[l, dec * hd:(dec + 1) * hd, :])
        out += jnp.dot(p_new, qkv[dec:dec + seen, 2 * hd:3 * hd], preferred_element_type=F32)
        attended[r0:r0 + rows, :] = out.astype(BF16)

    def remote(src, dst, send, recv, dev):
        return pltpu.make_async_remote_copy(src_ref=src, dst_ref=dst, send_sem=send, recv_sem=recv, device_id={"tp": dev}, device_id_type=MESH)

    def pair_copy(s):
        r0, rows = streams[s]
        return remote(part.at[pl.ds(other_base, ngrp), pl.ds(r0, rows)], pair_in.at[:, pl.ds(r0, rows)], pair_send.at[s], pair_recv.at[s], partner)

    met = []

    def project_out(s, lhs_ref, w_ref):
        r0, rows = streams[s]
        lhs = lhs_ref[r0:r0 + rows, :]
        step = min(4, ngrp)
        for base in (other_base, my_base):
            for c in range(0, ngrp, step):
                at = pl.multiple_of((base + c) * LANES, LANES)
                out = jnp.dot(lhs, w_ref[:, pl.ds(at, step * LANES)], preferred_element_type=F32).astype(BF16)
                for j in range(step):
                    part[base + c + j, r0:r0 + rows, :] = out[:, j * LANES:(j + 1) * LANES]
            if base is other_base:
                if not met:
                    met.append(True)
                    pl.semaphore_wait(barrier, chips)
                pair_copy(s).start()

    def block_at(s, group, half):
        r0, rows = streams[s]
        return group, pl.ds(pl.multiple_of(r0 + half * (rows // 2), rows // 2), rows // 2)

    own_group, own_half = lax.rem(chip, ngrp), chip // ngrp
    targets = [[block_at(s, group, half) for _, _, group, half in peers] for s in range(len(streams))]

    def own_rows(s):
        r0, rows = streams[s]
        return pl.ds(r0 // 2, rows // 2)

    loaded = set()

    def need(l, *names):
        for name in names:
            if (l, name) not in loaded:
                loaded.add((l, name))
                if l > 0 and name not in ("q", "k", "v"):
                    prefetch(1 << 40)
                load(l, name).wait()

    def start_compute(s, phase):
        l = phase // 2
        r0, rows = streams[s]
        norm(s, l + layers * (phase % 2))
        if phase % 2 == 0:
            need(l, "q", "k", "v")
            project_qkv(s, l)
        else:
            need(l, "gate", "up")
            a = normed[r0:r0 + rows, :]
            gate = jnp.dot(a, wg[l], preferred_element_type=F32)
            up = jnp.dot(a, wu[l], preferred_element_type=F32)
            act[r0:r0 + rows, :] = (gate * lax.logistic(gate) * up).astype(BF16)

    def end_compute(s, phase):
        l = phase // 2
        if phase % 2 == 0:
            if s >= decode_streams:
                need(l, "pre_keys", "pre_values")
                prefill_attention(s, l)
            else:
                decode_values(s, l)
            need(l, "o")
            project_out(s, attended, wo.at[l])
        else:
            need(l, "down")
            project_out(s, act, wd.at[l])

    def scatter(s):
        r0, rows = streams[s]
        pair_copy(s).wait()
        both = part[pl.ds(my_base, ngrp), r0:r0 + rows, :].astype(F32) + pair_in[:, r0:r0 + rows, :].astype(F32)
        mine[:, r0:r0 + rows, :] = both.astype(BF16)
        slot = own_rows(s)

        for (_, device, _, _), block in zip(peers, targets[s]):
            remote(mine.at[block], rs_in.at[chip, slot], rs_send.at[s], rs_recv.at[s], device).start()
        rs_in[chip, slot, :] = mine[(*block_at(s, own_group, own_half), slice(None))]

    def peer_blocks(s, send, recv):
        blocks = rs_in.at[pl.ds(0, chips - 1), own_rows(s)]
        return remote(blocks, blocks, send.at[s], recv.at[s], partner)

    def spread(s):
        group, rows = block_at(s, own_group, own_half)
        own = hbuf.at[my_base + group, rows]
        peer_blocks(s, rs_send, rs_recv).wait_recv()
        total = jnp.sum(rs_in[:, own_rows(s), :].astype(F32), axis=0) + hbuf[my_base + group, rows, :].astype(F32)
        hbuf[my_base + group, rows, :] = total.astype(BF16)
        for _, device, _, _ in peers:
            remote(own, own, ag_send.at[s], ag_recv.at[s], device).start()

    def hand_on(s):
        r0, rows = streams[s]
        blocks = hbuf.at[pl.ds(my_base, ngrp), pl.ds(r0, rows)]
        return remote(blocks, blocks, fwd_send.at[s], fwd_recv.at[s], partner)

    def forward(s):
        peer_blocks(s, ag_send, ag_recv).wait_recv()
        hand_on(s).start()

    def finish(s):
        peer_blocks(s, rs_send, rs_recv).wait_send()
        peer_blocks(s, ag_send, ag_recv).wait_send()
        hand_on(s).wait()

    phases = 2 * layers
    stages = {"start": start_compute, "middle": lambda s, phase: decode_logits(s, phase // 2), "end": end_compute, "scatter": lambda s, _: scatter(s), "spread": lambda s, _: spread(s),
              "forward": lambda s, _: forward(s), "finish": lambda s, _: finish(s)}
    order = stage_order(streams, decode_streams, phases)
    settled = max(i for i, (s, name, phase) in enumerate(order) if s < decode_streams and name == "end" and phase == 0)
    for i, (s, name, phase) in enumerate(order):
        if i > settled:
            prefetch(PACE[name])
        stages[name](s, phase)
        if name == "finish" and phase == phases - 1:
            r0, rows = streams[s]

            for c in range(ncol):
                out_ref[r0:r0 + rows, c * LANES:(c + 1) * LANES] = hbuf[c, r0:r0 + rows, :]


def solution(mesh):
    col_spec = P(None, None, "tp")
    row_spec = P(None, "tp", None)
    cache_spec = P(None, "dp", "tp", None, None)
    in_specs = (P("dp", None), P("dp"), P(), col_spec, col_spec, col_spec, row_spec, P(), col_spec, col_spec, row_spec, cache_spec, cache_spec)
    n = mesh.shape["tp"]

    def body(x, lengths, attn_gain, w_q, w_k, w_v, w_o, mlp_gain, w_gate, w_up, w_down, k_cache, v_cache):
        tok, width = x.shape
        layers, rows, _, seq, hd = k_cache.shape
        dec, ff, chips = rows - 1, w_gate.shape[-1], n // 2
        half, ncol, count = tok // 2, width // LANES, DECODE_STREAMS + PREFILL_STREAMS

        def flat(cache):
            return jnp.swapaxes(cache, 3, 4).reshape(layers, rows * hd, seq)

        def turned(w):
            return jnp.swapaxes(w, 1, 2)

        dma = pltpu.SemaphoreType.DMA
        vmem, hbm, smem = (pl.BlockSpec(memory_space=m) for m in (pltpu.VMEM, pltpu.HBM, pltpu.SMEM))
        return pl.pallas_call(
            functools.partial(layers_kernel, (n, layers, tok, width, dec, seq, hd, ff)),
            out_shape=jax.ShapeDtypeStruct((tok, width), BF16),
            in_specs=[smem, vmem, vmem] + [hbm] * 10,
            out_specs=vmem,
            scratch_shapes=[
                pltpu.VMEM((ncol, tok, LANES), BF16),
                pltpu.VMEM((ncol, tok, LANES), BF16),
                pltpu.VMEM((ncol // 2, tok, LANES), BF16),
                pltpu.VMEM((ncol // 2, tok, LANES), BF16),
                pltpu.VMEM((chips, half, LANES), BF16),
                pltpu.VMEM((tok, width), BF16),
                pltpu.VMEM((tok, 3 * hd), BF16),
                pltpu.VMEM((dec, BLOCK * hd), BF16),
                pltpu.VMEM((dec, seq), F32),
                pltpu.VMEM((dec, seq), BF16),
                pltpu.VMEM((dec, hd), F32),
                pltpu.VMEM((tok, hd), BF16),
                pltpu.VMEM((tok, ff), BF16),
                pltpu.VMEM((tok, LANES), F32),
                pltpu.VMEM((tok, LANES), F32),
                pltpu.VMEM((dec, LANES), jnp.int32),
                pltpu.VMEM((2 * layers, ncol, 1, LANES), F32),
                pltpu.VMEM((layers, 3 * hd, width), BF16),
                pltpu.VMEM((layers, hd, width), BF16),
                pltpu.VMEM((layers, width, ff), BF16),
                pltpu.VMEM((layers, width, ff), BF16),
                pltpu.VMEM((layers, ff, width), BF16),
                pltpu.VMEM((layers, rows * hd, seq), BF16),
                pltpu.VMEM((layers, rows * hd, seq), BF16),
                dma((ncol,)),
                dma((layers, 9 + 2 * DECODE_STREAMS)),
                dma((count,)), dma((count,)), dma((count,)), dma((count,)), dma((count,)), dma((count,)), dma((count,)), dma((count,)),
            ],
            compiler_params=pltpu.CompilerParams(collective_id=0, has_side_effects=True, vmem_limit_bytes=63 * 2**20),
        )(lengths, attn_gain, mlp_gain, x, turned(w_q), turned(w_k), turned(w_v), w_o, w_gate, w_up, w_down, flat(k_cache), flat(v_cache))

    return jax.shard_map(body, mesh=mesh, in_specs=in_specs, out_specs=P("dp", None), check_vma=False)
```

time: 91.4 us -> 79.7 us (0.87)
  Pallas kernels: 89.1 us -> 77.4 us
    pallas_call x1, Pallas kernels: 89.1 us -> 77.4 us  [body(): pl.pallas_call(functools.partial(layers_kernel, (n, layers, tok, width, d...]
where the time goes in v3:
time: 79.7 us; the launch traced here: 79.5 us
  Pallas kernels  77.4 us (97%)
  local copies, waits for them, and re-layouts  2.09 us (3%)
    pallas_call x1, Pallas kernels, body(): pl.pallas_call(functools.partial(layers_kernel, (n, layers, tok, width, d...  77.4 us
    unnamed x1, local copies, waits for them, and re-layouts  2.09 us

profile of v3, /device:TPU:97, one launch (start us, length us, event | category | flops | bytes accessed | tf_op | source)
XLA Modules:
  0.0 79.5 jit_solution(6929486223896190945)
XLA Ops:
  0.0 77.4 %shard_map.127 = bf16[192,2048]{1,0:T(8,128)(2,1)} custom-call(s32[65]{0:T(128)} %len_ref.1, bf16[2,2048]{1,0:T(2,128)(2,1)} %again_ref.1, bf16[2,2048]{1,0:T(2,128)(2,1)} %mgain_ref.1, bf16[192,2048]{1,0:T(8,128)(2,1)} %x_hbm.1, bf16[2,64,2048]{2,1,0:T(8,128)(2,1)} %bitcast.11, bf16[2,64,2048]{2,1,0:T(8,128)(2,1)} %bitcast.12, ...), custom_call_target="tpu_custom_call" | custom-call | tf_op jit(solution)/shard_map/pallas_call | solution.py:384
  77.4 2.1 %copy.15 = bf16[192,2048]{1,0:T(8,128)(2,1)} copy(bf16[192,2048]{1,0:T(8,128)(2,1)} %shard_map.127) | data formatting | bytes 1572864

commit v4 on v3

--- a/solution.py
+++ b/solution.py
@@ -14,10 +14,10 @@
 SUBLANES = 8
 BLOCK = 16
 DECODE_STREAMS, PREFILL_STREAMS = 2, 2
-ORDER = (3, 0, 0, 1, 2, 0, 3, 0, 2, 3, 1, 2, 1, 0, 1, 3, 2, 0, 0, 0, 0, 3, 0, 2, 3, 1, 3, 3, 2, 2, 2, 3, 2, 0, 1, 1, 1, 3, 1, 2, 0, 1, 0, 0, 0, 0, 3, 2, 1, 0, 3, 3, 2, 2, 3, 2, 3, 1, 0, 2, 1, 1, 1, 1, 3, 1, 2, 0, 0, 3, 1, 2, 3, 0, 3, 3, 2, 0, 2, 3, 2, 1, 2, 1, 1, 1, 0, 1, 3, 2, 0, 1, 2, 0, 3, 1, 3, 2, 0, 1)
+ORDER = (1, 2, 0, 0, 3, 0, 2, 0, 3, 2, 1, 3, 1, 0, 1, 2, 3, 0, 1, 0, 0, 2, 0, 3, 0, 2, 2, 2, 3, 3, 1, 3, 2, 3, 1, 1, 0, 1, 1, 2, 3, 0, 1, 0, 0, 0, 2, 0, 3, 2, 2, 2, 1, 3, 3, 3, 0, 2, 1, 1, 3, 1, 1, 0, 1, 2, 3, 1, 0, 2, 3, 0, 0, 0, 2, 2, 2, 3, 1, 3, 3, 2, 0, 1, 1, 1, 3, 1, 2, 0, 3, 1, 0, 2, 3, 0, 1, 2, 3, 1)
 MIB = 2**20
 PIECE = MIB // 2
-PACE = {"start": 2 * MIB, "middle": 4 * MIB, "end": 2 * MIB, "scatter": MIB // 2, "spread": MIB // 2, "forward": 0, "finish": 0}
+PACE = {"start": 2 * MIB, "middle": 4 * MIB, "end": MIB, "scatter": 0, "spread": 0, "forward": 0, "finish": 0}
 F32 = jnp.float32
 BF16 = jnp.bfloat16
 
@@ -46,7 +46,7 @@
 def layers_kernel(dims, len_ref, again_ref, mgain_ref, x_hbm, wq_hbm, wk_hbm, wv_hbm, wo_hbm, wg_hbm, wu_hbm, wd_hbm, kc_hbm, vc_hbm, out_ref,
                   hbuf, part, pair_in, mine, rs_in, normed, qkv, qbd, logits, probs, v_self, attended, act, cos_ref, sin_ref, len_col, gains,
                   wqkv, wo, wg, wu, wd, kc, vc,
-                  x_sem, w_sem, pair_send, pair_recv, rs_send, rs_recv, ag_send, ag_recv, fwd_send, fwd_recv):
+                  x_sem, w_sem, pair_send, pair_recv, rs_send, rs_recv, ag_send, ag_recv, fwd_send, fwd_recv, out_sem):
     n, layers, tok, width, dec, seq, hd, ff = dims
     chips = n // 2
     side = int(round(chips ** 0.5))
@@ -357,7 +357,9 @@
             r0, rows = streams[s]
 
             for c in range(ncol):
-                out_ref[r0:r0 + rows, c * LANES:(c + 1) * LANES] = hbuf[c, r0:r0 + rows, :]
+                pltpu.make_async_copy(hbuf.at[c, pl.ds(r0, rows)], out_ref.at[pl.ds(r0, rows), pl.ds(c * LANES, LANES)], out_sem.at[s]).start()
+    for s, (r0, rows) in enumerate(streams):
+        pltpu.make_async_copy(normed.at[pl.ds(r0, rows)], out_ref.at[pl.ds(r0, rows)], out_sem.at[s]).wait()
 
 
 def solution(mesh):
@@ -385,7 +387,7 @@
             functools.partial(layers_kernel, (n, layers, tok, width, dec, seq, hd, ff)),
             out_shape=jax.ShapeDtypeStruct((tok, width), BF16),
             in_specs=[smem, vmem, vmem] + [hbm] * 10,
-            out_specs=vmem,
+            out_specs=hbm,
             scratch_shapes=[
                 pltpu.VMEM((ncol, tok, LANES), BF16),
                 pltpu.VMEM((ncol, tok, LANES), BF16),
@@ -413,7 +415,7 @@
                 pltpu.VMEM((layers, rows * hd, seq), BF16),
                 dma((ncol,)),
                 dma((layers, 9 + 2 * DECODE_STREAMS)),
-                dma((count,)), dma((count,)), dma((count,)), dma((count,)), dma((count,)), dma((count,)), dma((count,)), dma((count,)),
+                *[dma((count,)) for _ in range(9)],
             ],
             compiler_params=pltpu.CompilerParams(collective_id=0, has_side_effects=True, vmem_limit_bytes=63 * 2**20),
         )(lengths, attn_gain, mlp_gain, x, turned(w_q), turned(w_k), turned(w_v), w_o, w_gate, w_up, w_down, flat(k_cache), flat(v_cache))

time: 79.7 us -> 79.3 us (level)
  no operation moved by 1% of the time
where the time goes in v4:
time: 79.3 us; the launch traced here: 79.1 us
  Pallas kernels  77 us (97%)
  local copies, waits for them, and re-layouts  2.09 us (3%)
    pallas_call x1, Pallas kernels, body(): pl.pallas_call(functools.partial(layers_kernel, (n, layers, tok, width, d...  77 us
    unnamed x1, local copies, waits for them, and re-layouts  2.09 us

profile of v4, /device:TPU:97, one launch (start us, length us, event | category | flops | bytes accessed | tf_op | source)
XLA Modules:
  0.0 79.1 jit_solution(4047349469882879840)
XLA Ops:
  0.0 77.0 %shard_map.127 = bf16[192,2048]{1,0:T(8,128)(2,1)} custom-call(s32[65]{0:T(128)} %len_ref.1, bf16[2,2048]{1,0:T(2,128)(2,1)} %again_ref.1, bf16[2,2048]{1,0:T(2,128)(2,1)} %mgain_ref.1, bf16[192,2048]{1,0:T(8,128)(2,1)} %x_hbm.1, bf16[2,64,2048]{2,1,0:T(8,128)(2,1)} %bitcast.11, bf16[2,64,2048]{2,1,0:T(8,128)(2,1)} %bitcast.12, ...), custom_call_target="tpu_custom_call" | custom-call | tf_op jit(solution)/shard_map/pallas_call | solution.py:386
  77.0 2.1 %copy.15 = bf16[192,2048]{1,0:T(8,128)(2,1)} copy(bf16[192,2048]{1,0:T(8,128)(2,1)} %shard_map.127) | data formatting | bytes 1572864
